TPU v7x, 32 devices: a whole 2x2x4 slice. The times are simulated.
32 devices in a mesh: dp: 8 (over z, y), section: 4 (over x, core).
Axes of the slice: x: 2, y: 2, z: 4, core: 2. Of those that a mesh axis runs over, the one named last changes fastest.
Arguments:
- slot_of_token: int32 [2, 1, 1024], P(None, None, 'dp'), may hold values from -1 to 127, as said below
- gate_prob: float32 [2, 1, 1024], P(None, None, 'dp'), may hold values from 0.2 to 1
- layer_input: bfloat16 [1, 1024, 7168], P(None, 'dp', 'section'), may hold values from -6 to 6
- preact: bfloat16 [1, 1024, 2048], P(None, 'dp', 'section'), may hold values from -6 to 6
- top_grad: bfloat16 [1, 1024, 3584], P(None, 'dp'), may hold values from -6 to 6
- w_up: bfloat16 [1024, 7168], P('dp', 'section'), may hold values from -0.09375 to 0.09375
- w_down: bfloat16 [1024, 7168], P('dp', 'section'), may hold values from -0.1875 to 0.1875
Outputs:
- grad_inputs: bfloat16 [1, 1024, 7168], P(None, 'dp', 'section')
- grad_up: float32 [1024, 7168], P('dp', 'section')
- grad_down: float32 [1024, 7168], P('dp', 'section')
Inputs may be any that keep to these rules, and one draw needn't show every extreme that they name: `slot_of_token`: within one layer, one micro-batch and the 128 tokens of one data replica, the values other than -1 are distinct; -1 marks a token that is not routed to the expert or dropped.
All inputs are finite; a program needn't handle non-finite values.
Results may differ from a plain program's by a relative error of at most 0.0098.
Values may be sent and summed in bfloat16 or wider, within the bound.
A program may use at most 128 MiB of HBM per device.

v0:
```python
import jax
import jax.numpy as jnp
from jax import lax
from jax.sharding import PartitionSpec as P


def swapped(block, axis, apart):
    count = lax.axis_size(axis)
    route = []
    for low in range(count):
        high = low | 1 << apart
        if high != low and high < count:
            route += [(low, high), (high, low)]
    return lax.ppermute(block, axis, route)


def passed_along(shard, axis, by):
    count = lax.axis_size(axis)
    pairs = [(i, i + by) for i in range(count) if 0 <= i + by < count]
    return lax.ppermute(shard, axis, pairs)


def silu_slope(pre):
    sigmoid_val = jax.nn.sigmoid(pre)
    return sigmoid_val * (1.0 + pre * (1.0 - sigmoid_val))


def pick(stack, index):
    return lax.dynamic_index_in_dim(stack, index, 0, keepdims=False)


def local(slot_of_token, gate_prob, layer_input, preact, top_grad, w_up, w_down):
    micro_count = layer_input.shape[0]
    token_rows = layer_input.shape[1]
    half_width = layer_input.shape[2]
    slot_count = preact.shape[1]
    section_index = lax.axis_index("section")
    pair_index = section_index // 2
    core_index = section_index % 2
    layer_count = lax.axis_size("section") // 2
    up_half, down_half = (
        lax.all_gather(w_up, "dp", axis=0, tiled=True),
        lax.all_gather(w_down, "dp", axis=0, tiled=True),
    )
    hidden_units = up_half.shape[0]
    other_pre = swapped(preact, "section", 0)
    pre_full = jnp.where(
        core_index == 0,
        jnp.concatenate([preact, other_pre], 2),
        jnp.concatenate([other_pre, preact], 2),
    ).astype(jnp.float32)
    slope_all = silu_slope(pre_full)
    hidden_all = jax.nn.silu(pre_full).astype(jnp.bfloat16)
    slots_here = pick(slot_of_token, pair_index)
    gates_here = pick(gate_prob, pair_index)
    slot_ids = jnp.arange(slot_count, dtype=jnp.int32)
    onehot_all = (slots_here[:, None, :] == slot_ids[None, :, None]).astype(jnp.bfloat16)
    slot_inputs = jnp.einsum(
        "mst,mtd->msd", onehot_all, layer_input, preferred_element_type=jnp.float32
    ).astype(jnp.bfloat16)
    top_half = lax.dynamic_slice_in_dim(top_grad, core_index * half_width, half_width, 2)
    tick_count = micro_count + layer_count - 1
    received = jnp.zeros((token_rows, half_width), jnp.bfloat16)
    grad_inputs = jnp.zeros_like(layer_input)
    pre_grads = jnp.zeros((micro_count, slot_count, hidden_units), jnp.bfloat16)
    slot_grads = jnp.zeros((micro_count, slot_count, half_width), jnp.bfloat16)
    for step_index in range(tick_count):
        micro_raw = step_index - (layer_count - 1 - pair_index)
        active = (micro_raw >= 0) & (micro_raw < micro_count)
        micro_now = jnp.clip(micro_raw, 0, micro_count - 1)
        incoming = jnp.where(pair_index == layer_count - 1, pick(top_half, micro_now), received)
        onehot = pick(onehot_all, micro_now)
        scaled = (pick(gates_here, micro_now)[:, None] * incoming.astype(jnp.float32)).astype(
            jnp.bfloat16
        )
        slot_grad = jnp.dot(onehot, scaled, preferred_element_type=jnp.float32).astype(jnp.bfloat16)
        partial_grad = lax.dot_general(
            slot_grad, down_half, (((1,), (1,)), ((), ())), preferred_element_type=jnp.float32
        )
        other_grad = swapped(partial_grad, "section", 0)
        hidden_grad = partial_grad + other_grad
        pre_grad = (hidden_grad * pick(slope_all, micro_now)).astype(jnp.bfloat16)
        slot_input_grad = jnp.dot(pre_grad, up_half, preferred_element_type=jnp.float32).astype(
            jnp.bfloat16
        )
        delta = lax.dot_general(
            onehot, slot_input_grad, (((0,), (0,)), ((), ())), preferred_element_type=jnp.float32
        )
        grad_new = (incoming.astype(jnp.float32) + delta).astype(jnp.bfloat16)
        grad_inputs = lax.dynamic_update_index_in_dim(
            grad_inputs, jnp.where(active, grad_new, pick(grad_inputs, micro_now)), micro_now, 0
        )
        pre_grads = lax.dynamic_update_index_in_dim(
            pre_grads, jnp.where(active, pre_grad, pick(pre_grads, micro_now)), micro_now, 0
        )
        slot_grads = lax.dynamic_update_index_in_dim(
            slot_grads, jnp.where(active, slot_grad, pick(slot_grads, micro_now)), micro_now, 0
        )
        received = passed_along(grad_new, "section", -2)
    up_rows = jnp.einsum("msf,msd->fd", pre_grads, slot_inputs, preferred_element_type=jnp.float32)
    down_rows = jnp.einsum(
        "msf,msd->fd", hidden_all, slot_grads, preferred_element_type=jnp.float32
    )
    summed = lax.psum_scatter(
        jnp.concatenate([up_rows, down_rows], 1), "dp", scatter_dimension=0, tiled=True
    )
    grad_up = summed[:, :half_width]
    grad_down = summed[:, half_width:]
    return (grad_inputs, grad_up, grad_down)


def solution(mesh):
    in_specs = (
        P(None, None, "dp"),
        P(None, None, "dp"),
        P(None, "dp", "section"),
        P(None, "dp", "section"),
        P(None, "dp", None),
        P("dp", "section"),
        P("dp", "section"),
    )
    out_specs = (P(None, "dp", "section"), P("dp", "section"), P("dp", "section"))
    return jax.shard_map(local, mesh=mesh, in_specs=in_specs, out_specs=out_specs, check_vma=False)
```

profile of v0, /device:TPU:2, one launch (start us, length us, event | category | flops | bytes accessed | tf_op | source)
XLA Modules:
  0.0 431.9 jit_solution(3888123693103680271)
XLA Ops:
  7.2 0.0 copy-start
  7.2 0.0 copy-start.4
  7.2 0.0 all-gather.3.cloned.1.call-start
  7.2 0.7 all-gather.3.cloned.1.call-update
  7.9 0.0 all-gather.5.cloned.1.call-start
  8.0 0.7 all-gather.5.cloned.1.call-update
  8.7 0.0 copy-start.1
  8.7 0.0 reduce-scatter.2.cloned.1.call-start
  8.8 0.7 fusion.44
  9.5 0.7 fusion.45
  10.1 1.4 convolution_convert_fusion.4
  11.5 66.1 %all-gather.3.cloned.1.call-done = bf16[1024,1792]{1,0:T(8,128)(2,1)} async-done(((bf16[128,1792]{1,0:T(8,128)(2,1)}), bf16[1024,1792]{1,0:T(8,128)(2,1)}) %all-gather.3.cloned.1.call-update) | async-done | bytes 3670032 | tf_op jit(solution)/shard_map/all_gather | solution.py:43
  77.7 3.3 fusion.51
  81.0 0.1 collective-permute-start
  81.1 0.0 copy-done.4
  81.1 0.5 collective-permute-start.1
  81.6 1.6 collective-permute-done.1
  83.2 0.0 copy-start.6
  83.2 0.0 collective-permute-done
  83.2 1.3 multiply_convert_fusion.2
  84.5 60.3 %all-gather.5.cloned.1.call-done = bf16[1024,1792]{1,0:T(8,128)(2,1)} async-done(((bf16[128,1792]{1,0:T(8,128)(2,1)}), bf16[1024,1792]{1,0:T(8,128)(2,1)}) %all-gather.5.cloned.1.call-update) | async-done | bytes 3670032 | tf_op jit(solution)/shard_map/all_gather | solution.py:42
  144.8 0.0 copy-done.1
  144.8 2.9 fusion
  147.7 2.5 collective-permute-start.2
  150.2 0.0 copy-done.6
  150.2 8.1 %collective-permute-done.2 = bf16[128,1792]{1,0:T(8,128)(2,1)S(1)} collective-permute-done((bf16[128,1792]{1,0:T(8,128)(2,1)S(1)}, bf16[128,1792]{1,0:T(8,128)(2,1)S(1)}, u32[]{:S(2)}, u32[]{:S(2)}) %collective-permute-start.2) | collective-permute-done | bytes 458784 | tf_op jit(solution)/shard_map/ppermute | solution.py:20
  158.3 0.0 copy-start.2
  158.3 0.8 copy-done.2
  159.1 0.3 convolution_convert_fusion.3
  159.4 3.3 fusion.52
  162.7 0.1 collective-permute-start.3
  162.8 0.0 copy-start.5
  162.8 0.0 copy-start.7
  162.9 5.3 %fusion.17 = f32[1024,1792]{1,0:T(8,128)} fusion(bf16[128,1792]{1,0:T(8,128)(2,1)S(1)} %convolution_convert_fusion.3, bf16[128,1792]{1,0:T(8,128)(2,1)S(1)} %convolution_convert_fusion.4, pred[]{:T(512)S(6)} %and.20, pred[]{:T(512)S(6)} %and.18, bf16[128,512]{1,0:T(8,128)(2,1)} %bitcast.37, bf16[128,512]{1,0:T(8,128)(2,1)} %bitcast.33, pred[]{:T(512)S(6)} %eq.36), kind=kOutput, calls=%fused_computation.31 | convolution fusion | flops 472186880 | bytes 8519683 | tf_op jit(solution)/shard_map/msf,msd->fd/dot_general | solution.py:101
  168.1 0.0 collective-permute-done.3
  168.1 0.0 copy-done.5
  168.1 0.0 copy-done.7
  168.2 1.3 multiply_convert_fusion.1
  169.4 0.0 copy-done
  169.4 4.3 fusion.4
  173.7 10.7 %pad_maximum_fusion = f32[1024,3584]{1,0:T(8,128)} fusion(f32[1024,1792]{1,0:T(8,128)} %fusion.17, f32[1024,1792]{1,0:T(8,128)} %fusion.4), kind=kLoop, calls=%fused_computation | loop fusion | flops 3670016 | bytes 29360128 | tf_op jit(solution)/shard_map/concatenate | solution.py:105
  184.4 0.0 copy-start.3
  184.4 0.0 reduce-scatter.2.cloned.1.call-update
  184.4 1.0 copy-done.3
  185.4 3.7 fusion.3
  189.1 233.5 %reduce-scatter.2.cloned.1.call-done = f32[128,3584]{1,0:T(8,128)} async-done(((f32[1024,3584]{1,0:T(8,128)}), f32[128,3584]{1,0:T(8,128)}) %reduce-scatter.2.cloned.1.call-update) | async-done | bytes 1835024 | tf_op jit(solution)/shard_map/reduce_scatter | solution.py:104
  422.6 2.8 fusion.50
Async XLA Ops:
  7.2 162.3 %copy-start = (bf16[1,128,1792]{2,1,0:T(8,128)(2,1)S(1)}, bf16[1,128,1792]{2,1,0:T(8,128)(2,1)}, u32[]{:S(2)}) copy-start(bf16[1,128,1792]{2,1,0:T(8,128)(2,1)} %param.9) | copy-start | bytes 1376260
  7.2 73.9 %copy-start.4 = (bf16[1,128,512]{2,1,0:T(8,128)(2,1)S(1)}, bf16[1,128,512]{2,1,0:T(8,128)(2,1)}, u32[]{:S(2)}) copy-start(bf16[1,128,512]{2,1,0:T(8,128)(2,1)} %param.10) | copy-start | bytes 393220
  7.2 70.5 %all-gather.3.cloned.1.call-start = ((), (), s32[]{:S(2)}) async-start(), calls=%async_computation.1 | async-start | bytes 4128768 | tf_op jit(solution)/shard_map/all_gather | solution.py:43
  7.9 136.9 %all-gather.5.cloned.1.call-start = ((), (), s32[]{:S(2)}) async-start(), calls=%async_computation.2 | async-start | bytes 4128768 | tf_op jit(solution)/shard_map/all_gather | solution.py:42
  8.7 136.1 %copy-start.1 = (bf16[1,128,3584]{2,1,0:T(8,128)(2,1)S(1)}, bf16[1,128,3584]{2,1,0:T(8,128)(2,1)}, u32[]{:S(2)}) copy-start(bf16[1,128,3584]{2,1,0:T(8,128)(2,1)} %param.11) | copy-start | bytes 2752516
  8.7 413.9 %reduce-scatter.2.cloned.1.call-start = ((), (), s32[]{:S(2)}) async-start(), calls=%async_computation.3 | async-start | bytes 16515072 | tf_op jit(solution)/shard_map/reduce_scatter | solution.py:104
  81.0 2.2 collective-permute-start
  81.1 2.1 collective-permute-start.1
  83.2 67.0 %copy-start.6 = (bf16[1,128,512]{2,1,0:T(8,128)(2,1)}, bf16[1,128,512]{2,1,0:T(8,128)(2,1)S(1)}, u32[]{:S(2)}) copy-start(bf16[1,128,512]{2,1,0:T(8,128)(2,1)S(1)} %collective-permute-done.1) | copy-start | bytes 393220
  147.7 10.6 %collective-permute-start.2 = (bf16[128,1792]{1,0:T(8,128)(2,1)S(1)}, bf16[128,1792]{1,0:T(8,128)(2,1)S(1)}, u32[]{:S(2)}, u32[]{:S(2)}) collective-permute-start(bf16[128,1792]{1,0:T(8,128)(2,1)S(1)} %fusion), channel_id=1, source_target_pairs={{2,0},{3,1},{6,4},{7,5},{10,8},{11,9},{14,12},{15,13},{18,16},{19,... | collective-permute-start | bytes 1376264 | tf_op jit(solution)/shard_map/ppermute | solution.py:20
  158.3 0.8 copy-start.2
  162.7 5.4 %collective-permute-start.3 = (f32[128,1024]{1,0:T(8,128)S(1)}, f32[128,1024]{1,0:T(8,128)}, u32[]{:S(2)}, u32[]{:S(2)}) collective-permute-start(f32[128,1024]{1,0:T(8,128)S(1)} %fusion.52), channel_id=1, source_target_pairs={{0,1},{1,0},{2,3},{3,2},{4,5},{5,4},{6,7},{7,6},{8,9},{9,8},{10,11... | collective-permute-start | bytes 1572872 | tf_op jit(solution)/shard_map/ppermute | solution.py:14
  162.8 5.3 %copy-start.5 = (bf16[1,128,512]{2,1,0:T(8,128)(2,1)S(1)}, bf16[1,128,512]{2,1,0:T(8,128)(2,1)}, u32[]{:S(2)}) copy-start(bf16[1,128,512]{2,1,0:T(8,128)(2,1)} %param.10) | copy-start | bytes 393220
  162.8 5.3 %copy-start.7 = (bf16[1,128,512]{2,1,0:T(8,128)(2,1)S(1)}, bf16[1,128,512]{2,1,0:T(8,128)(2,1)}, u32[]{:S(2)}) copy-start(bf16[1,128,512]{2,1,0:T(8,128)(2,1)} %copy-done.6) | copy-start | bytes 393220
  184.4 1.0 copy-start.3
Sparse Core Ops, SparseCore 0:
  10.2 67.4 all-gather.2
  79.8 64.9 all-gather.4
  184.5 238.0 reduce-scatter.1
where the time goes:
time: 434 us; the launch traced here: 432 us
  waiting for transfers between devices  371 us (85%)
  matrix products  24.5 us (6%)
  between operations  13.9 us (3%)
  other arithmetic  13.3 us (3%)
  local copies, waits for them, and re-layouts  5.98 us (1%)
    reduce_scatter x1, waiting for transfers between devices, local(): lax.psum_scatter(jnp.concatenate([up_rows, down_rows], 1), 'dp', scatter_...  234 us
    all_gather x1, waiting for transfers between devices, local(): lax.all_gather(w_down, 'dp', axis=0, tiled=True)  66.1 us
    all_gather x1, waiting for transfers between devices, local(): lax.all_gather(w_up, 'dp', axis=0, tiled=True)  60.3 us
    concatenate x1, other arithmetic, local(): jnp.concatenate([up_rows, down_rows], 1)  10.7 us
  transfers between devices with their start and end apart: 7, of which 5 were waited for; matrix products, arithmetic and copies ran while one was open for 4% of the time, Pallas kernels for 0%

commit v1 on v0

v1 whole, which is shorter than its diff:
```python
import functools

import jax
import jax.numpy as jnp
from jax import lax
from jax.experimental import pallas as pl
from jax.experimental.pallas import tpu as pltpu
from jax.sharding import PartitionSpec as P

MESH = pl.DeviceIdType.MESH
BF16 = jnp.bfloat16
F32 = jnp.float32
NT = (((1,), (1,)), ((), ()))
TN = (((0,), (0,)), ((), ()))


def silu_slope(pre):
    sigmoid_val = jax.nn.sigmoid(pre)
    return sigmoid_val * (1.0 + pre * (1.0 - sigmoid_val))


class Gather:
    def __init__(self, buf, push_sem, fwd_sem, recv_sem, me, n):
        self.buf, self.push_sem, self.fwd_sem, self.recv_sem = buf, push_sem, fwd_sem, recv_sem
        self.me, self.n, self.half = me, n, n // 2
        self.mate = me + 1 - 2 * lax.rem(me, 2)

    def copy(self, block, to, sem):
        return pltpu.make_async_remote_copy(
            src_ref=self.buf.at[block], dst_ref=self.buf.at[block], send_sem=sem,
            recv_sem=self.recv_sem.at[block], device_id={"dp": to}, device_id_type=MESH,
        )

    def row(self, k):
        return lax.rem(self.me - 2 * k + 2 * self.n, self.n)

    def other(self, k):
        return lax.rem(self.mate - 2 * k + 2 * self.n, self.n)

    def push_copy(self, k):
        return self.copy(self.me, lax.rem(self.me + 2 * k, self.n), self.push_sem.at[k])

    def mate_copy(self):
        return self.copy(self.me, self.mate, self.push_sem.at[0])

    def fwd_copy(self, k):
        return self.copy(self.row(k), self.mate, self.fwd_sem.at[k])

    def push(self):
        self.mate_copy().start()

        @pl.loop(1, self.half)
        def _(k):
            self.push_copy(k).start()

    def wait_block(self, block):
        self.copy(block, self.mate, self.fwd_sem.at[0]).wait_recv()

    def forward(self):
        @pl.loop(1, self.half)
        def _(k):
            self.wait_block(self.row(k))
            self.fwd_copy(k).start()

    def drain(self):
        self.mate_copy().wait_send()

        @pl.loop(1, self.half)
        def _(k):
            self.push_copy(k).wait_send()
            self.fwd_copy(k).wait_send()


def kernel(
    n, layers, slot_row, slot_col, gate_col, x_ref, pre_ref, top_ref, up_ref, down_ref,
    gin_ref, gup_ref, gdown_ref,
    sg_all, up_all, xs_all, pre_all, slope_all, hid_all, part_mine, part_other, pg_all, pg_own, acc, inc,
    sg_push, sg_fwd, sg_recv, up_push, up_fwd, up_recv, xs_push, xs_fwd, xs_recv,
    pre_send, pre_recv, pre_mate_send, pre_mate_recv, part_send, part_recv, pg_send, pg_recv,
    down_send, down_recv,
):
    me = lax.axis_index("dp")
    sec = lax.axis_index("section")
    pair, core = sec // 2, lax.rem(sec, 2)
    twin = sec + 1 - 2 * core
    half_n = n // 2
    slots, half = x_ref.shape
    is_first = pair == layers - 1

    sg = Gather(sg_all, sg_push, sg_fwd, sg_recv, me, n)
    up = Gather(up_all, up_push, up_fwd, up_recv, me, n)
    xs = Gather(xs_all, xs_push, xs_fwd, xs_recv, me, n)

    barrier = pltpu.get_barrier_semaphore()

    @pl.loop(1, n)
    def _(k):
        pl.semaphore_signal(barrier, inc=1, device_id={"dp": lax.rem(me + k, n)}, device_id_type=MESH)

    pl.semaphore_signal(barrier, inc=1, device_id={"section": twin}, device_id_type=MESH)

    @pl.when(pair > 0)
    def _():
        pl.semaphore_signal(barrier, inc=1, device_id={"section": sec - 2}, device_id_type=MESH)

    @pl.when(pair < layers - 1)
    def _():
        pl.semaphore_signal(barrier, inc=1, device_id={"section": sec + 2}, device_id_type=MESH)

    onehot = (slot_row[...] == lax.broadcasted_iota(jnp.int32, (slots, slots), 0)).astype(BF16)

    def make_slot_grad():
        scaled = (gate_col[...] * inc[...].astype(F32)).astype(BF16)
        sg_all[me] = jnp.dot(onehot, scaled, preferred_element_type=F32).astype(BF16)

    @pl.when(is_first)
    def _():
        inc[...] = top_ref[:, pl.ds(pl.multiple_of(core * half, 128), half)]
        make_slot_grad()

    up_all[me] = up_ref[...]
    xs_all[me] = jnp.dot(onehot, x_ref[...], preferred_element_type=F32).astype(BF16)

    near_pairs = (pair > 0).astype(jnp.int32) + (pair < layers - 1).astype(jnp.int32)
    pl.semaphore_wait(barrier, n + near_pairs)

    @pl.when(is_first)
    def _():
        sg.push()

    owner_core = me // half_n

    def pre_copy(j):
        to = core * half_n + j
        return pltpu.make_async_remote_copy(
            src_ref=pre_ref.at[j], dst_ref=pre_all.at[me], send_sem=pre_send.at[j],
            recv_sem=pre_recv.at[me], device_id={"dp": to}, device_id_type=MESH,
        )

    def pre_mate_copy():
        return pltpu.make_async_remote_copy(
            src_ref=pre_all, dst_ref=pre_all, send_sem=pre_mate_send.at[0],
            recv_sem=pre_mate_recv.at[0], device_id={"section": twin}, device_id_type=MESH,
        )

    @pl.when(owner_core == core)
    def _():
        pre_all[me] = pre_ref[me - core * half_n]

    @pl.loop(0, half_n)
    def _(j):
        @pl.when(core * half_n + j != me)
        def _():
            pre_copy(j).start()

    up.push()

    def take_pre():
        @pl.when(owner_core == core)
        def _():
            @pl.loop(1, n)
            def _(k):
                src = lax.rem(me + k, n)
                pltpu.make_async_remote_copy(
                    src_ref=pre_ref.at[0], dst_ref=pre_all.at[src], send_sem=pre_send.at[0],
                    recv_sem=pre_recv.at[src], device_id={"dp": src}, device_id_type=MESH,
                ).wait_recv()

            pre_mate_copy().start()

        @pl.when(owner_core != core)
        def _():
            pre_mate_copy().wait_recv()

        @pl.loop(0, n)
        def _(b):
            pre = pre_all[b].astype(F32)
            slope_all[b] = silu_slope(pre)
            hid_all[b] = jax.nn.silu(pre).astype(BF16)

    def down_copy():
        return pltpu.make_async_remote_copy(
            src_ref=gin_ref, dst_ref=inc, send_sem=down_send.at[0],
            recv_sem=down_recv.at[0], device_id={"section": sec - 2}, device_id_type=MESH,
        )

    @pl.when(jnp.logical_not(is_first))
    def _():
        xs.push()
        take_pre()
        up.forward()
        xs.forward()
        pltpu.make_async_remote_copy(
            src_ref=gin_ref, dst_ref=inc, send_sem=down_send.at[0],
            recv_sem=down_recv.at[0], device_id={"section": sec + 2}, device_id_type=MESH,
        ).wait_recv()
        make_slot_grad()
        sg.push()

    def part_copy(b):
        return pltpu.make_async_remote_copy(
            src_ref=part_mine.at[b], dst_ref=part_other.at[b], send_sem=part_send.at[b],
            recv_sem=part_recv.at[b], device_id={"section": twin}, device_id_type=MESH,
        )

    def part_of(b):
        part_mine[b] = lax.dot_general(sg_all[b], down_ref[...], NT, preferred_element_type=F32)
        part_copy(b).start()

    def pg_copy(b):
        return pltpu.make_async_remote_copy(
            src_ref=pg_all.at[b], dst_ref=pg_own.at[me], send_sem=pg_send.at[b],
            recv_sem=pg_recv.at[me], device_id={"dp": b}, device_id_type=MESH,
        )

    def finish_of(b):
        part_copy(b).wait_recv()
        pg_all[b] = ((part_mine[b] + part_other[b]) * slope_all[b]).astype(BF16)

        @pl.when(b == me)
        def _():
            pg_own[me] = pg_all[me]

        @pl.when(b != me)
        def _():
            pg_copy(b).start()

    part_of(me)

    @pl.loop(1, half_n)
    def _(k):
        sg.wait_block(sg.row(k))
        sg.fwd_copy(k).start()
        part_of(sg.row(k))

    @pl.when(is_first)
    def _():
        take_pre()

    @pl.loop(0, half_n)
    def _(k):
        finish_of(sg.row(k))

    @pl.loop(0, half_n)
    def _(k):
        sg.wait_block(sg.other(k))
        part_of(sg.other(k))
        finish_of(sg.other(k))

    @pl.when(is_first)
    def _():
        up.forward()
        xs.push()

    def wait_pg(b):
        pltpu.make_async_remote_copy(
            src_ref=pg_all.at[b], dst_ref=pg_own.at[b], send_sem=pg_send.at[b],
            recv_sem=pg_recv.at[b], device_id={"dp": b}, device_id_type=MESH,
        ).wait_recv()

    acc[...] = jnp.dot(pg_own[me], up_all[me], preferred_element_type=F32)

    @pl.loop(1, half_n)
    def _(k):
        b = up.row(k)
        wait_pg(b)
        acc[...] += jnp.dot(pg_own[b], up_all[b], preferred_element_type=F32)

    @pl.loop(0, half_n)
    def _(k):
        b = up.other(k)
        up.wait_block(b)
        wait_pg(b)
        acc[...] += jnp.dot(pg_own[b], up_all[b], preferred_element_type=F32)

    onehot_t = (slot_col[...] == lax.broadcasted_iota(jnp.int32, (slots, slots), 1)).astype(BF16)
    delta = jnp.dot(onehot_t, acc[...].astype(BF16), preferred_element_type=F32)
    gin_ref[...] = (inc[...].astype(F32) + delta).astype(BF16)

    @pl.when(pair > 0)
    def _():
        down_copy().start()

    @pl.when(is_first)
    def _():
        xs.forward()

    def weight_grad(out_ref, left, right):
        out_ref[...] = lax.dot_general(left[0], right[0], TN, preferred_element_type=F32)

        @pl.loop(1, n)
        def _(b):
            out_ref[...] += lax.dot_general(left[b], right[b], TN, preferred_element_type=F32)

    weight_grad(gdown_ref, hid_all, sg_all)

    @pl.loop(0, half_n)
    def _(k):
        xs.wait_block(xs.other(k))

    weight_grad(gup_ref, pg_all, xs_all)

    sg.drain()
    up.drain()
    xs.drain()

    @pl.loop(0, half_n)
    def _(j):
        @pl.when(core * half_n + j != me)
        def _():
            pre_copy(j).wait_send()

    @pl.when(owner_core == core)
    def _():
        pre_mate_copy().wait_send()

    @pl.loop(0, n)
    def _(b):
        part_copy(b).wait_send()

        @pl.when(b != me)
        def _():
            pg_copy(b).wait_send()

    @pl.when(pair > 0)
    def _():
        down_copy().wait_send()


def local(n, layers, slot_of_token, gate_prob, layer_input, preact, top_grad, w_up, w_down):
    pair = lax.axis_index("section") // 2
    slots, half = layer_input.shape[1:]
    units = w_up.shape[0]
    slot_here = lax.dynamic_index_in_dim(slot_of_token, pair, 0, keepdims=False)
    gate_here = lax.dynamic_index_in_dim(gate_prob, pair, 0, keepdims=False)
    pre = preact[0].reshape(slots, n // 2, units).transpose(1, 0, 2)
    vmem = pl.BlockSpec(memory_space=pltpu.VMEM)
    dma = lambda count: pltpu.SemaphoreType.DMA((count,))
    wide = pltpu.VMEM((n, slots, half), BF16)
    thin = lambda dtype: pltpu.VMEM((n, slots, units), dtype)
    gin, gup, gdown = pl.pallas_call(
        functools.partial(kernel, n, layers),
        out_shape=[
            jax.ShapeDtypeStruct((slots, half), BF16),
            jax.ShapeDtypeStruct((units, half), F32),
            jax.ShapeDtypeStruct((units, half), F32),
        ],
        in_specs=[vmem] * 8,
        out_specs=[vmem] * 3,
        scratch_shapes=[
            wide, pltpu.VMEM((n, units, half), BF16), wide,
            thin(BF16), thin(F32), thin(BF16), thin(F32), thin(F32), thin(BF16), thin(BF16),
            pltpu.VMEM((slots, half), F32),
            pltpu.VMEM((slots, half), BF16),
            dma(n // 2), dma(n // 2), dma(n), dma(n // 2), dma(n // 2), dma(n), dma(n // 2), dma(n // 2), dma(n),
            dma(n // 2), dma(n), dma(1), dma(1), dma(n), dma(n), dma(n), dma(n),
            dma(1), dma(1),
        ],
        compiler_params=pltpu.CompilerParams(
            collective_id=0, has_side_effects=True, vmem_limit_bytes=62 * 1024 * 1024
        ),
    )(
        slot_here, slot_here.reshape(slots, 1), gate_here.reshape(slots, 1),
        layer_input[0], pre, top_grad[0], w_up, w_down,
    )
    return gin[None], gup, gdown


def solution(mesh):
    n, sections = mesh.shape["dp"], mesh.shape["section"]
    in_specs = (
        P(None, None, "dp"),
        P(None, None, "dp"),
        P(None, "dp", "section"),
        P(None, "dp", "section"),
        P(None, "dp", None),
        P("dp", "section"),
        P("dp", "section"),
    )
    out_specs = (P(None, "dp", "section"), P("dp", "section"), P("dp", "section"))
    return jax.shard_map(
        functools.partial(local, n, sections // 2), mesh=mesh, in_specs=in_specs, out_specs=out_specs, check_vma=False
    )
```

time: 434 us -> 218 us (0.50)
  the two profiles are of different devices: /device:TPU:2 before, /device:TPU:0 now
where the time goes in v1:
time: 218 us
  Pallas kernels  209 us (96%)
  local copies, waits for them, and re-layouts  8.6 us (4%)
    pallas_call x1, Pallas kernels, local(): pl.pallas_call(functools.partial(kernel, n, layers), out_shape=[jax.Shape...  209 us
    unnamed x12, local copies, waits for them, and re-layouts  5.1 us

profile of v1, /device:TPU:0, one launch (start us, length us, event | category | flops | bytes accessed | tf_op | source)
XLA Modules:
  0.0 218.2 jit_solution(10408960842374269736)
XLA Ops:
  0.6 0.0 copy-start
  0.6 0.0 copy-start.3
  0.7 0.6 copy-done
  1.3 1.2 fusion
  2.6 0.7 copy.14.slot_col
  3.3 0.7 copy.15.gate_col
  4.0 0.0 copy-done.3
  4.0 0.1 copy.12
  4.2 0.8 copy.13
  4.9 209.0 %shard_map.94 = (bf16[128,1792]{1,0:T(8,128)(2,1)}, f32[128,1792]{1,0:T(8,128)}, f32[128,1792]{1,0:T(8,128)}) custom-call(s32[1,128]{1,0:T(1,128)} %get-tuple-element.10.slot_row, s32[128,1]{1,0:T(8,128)} %copy.14.slot_col, f32[128,1]{1,0:T(8,128)} %copy.15.gate_col, bf16[128,1792]{1,0:T(8,128)(2,1)} %bitcast.15, bf16[4,128,128]{2,1,0:T(8,128)(2,1)} %bitcast.12, ...), custom_call_target="tpu_custom_call" | custom-call | tf_op jit(solution)/shard_map/pallas_call | solution.py:341
  213.9 0.0 copy-start.2
  213.9 1.9 copy.19
  215.8 0.0 copy-done.2
  215.8 0.0 copy-start.1
  215.8 0.9 copy.20
  216.7 0.6 copy-done.1
  217.3 0.9 copy.21
  (1 shorter events, 0.0 us)
Async XLA Ops:
  0.6 0.7 copy-start
  0.6 3.4 %copy-start.3 = (bf16[1,128,512]{2,1,0:T(8,128)(2,1)S(1)}, bf16[1,128,512]{2,1,0:T(8,128)(2,1)}, u32[]{:S(2)}) copy-start(bf16[1,128,512]{2,1,0:T(8,128)(2,1)} %param.10) | copy-start | bytes 393220
  213.9 1.9 copy-start.2
  215.8 1.5 copy-start.1

commit v2 on v1

--- a/solution.py
+++ b/solution.py
@@ -20,10 +20,11 @@
 
 
 class Gather:
-    def __init__(self, buf, push_sem, fwd_sem, recv_sem, me, n):
-        self.buf, self.push_sem, self.fwd_sem, self.recv_sem = buf, push_sem, fwd_sem, recv_sem
-        self.me, self.n, self.half = me, n, n // 2
-        self.mate = me + 1 - 2 * lax.rem(me, 2)
+    def __init__(self, buf, right_sem, left_sem, mate_sem, recv_sem, me, n):
+        self.buf, self.recv_sem = buf, recv_sem
+        self.right_sem, self.left_sem, self.mate_sem = right_sem, left_sem, mate_sem
+        self.me, self.last, self.at, self.side = me, n // 2 - 1, me // 2, lax.rem(me, 2)
+        self.mate = me + 1 - 2 * self.side
 
     def copy(self, block, to, sem):
         return pltpu.make_async_remote_copy(
@@ -31,51 +32,95 @@
             recv_sem=self.recv_sem.at[block], device_id={"dp": to}, device_id_type=MESH,
         )
 
-    def row(self, k):
-        return lax.rem(self.me - 2 * k + 2 * self.n, self.n)
-
-    def other(self, k):
-        return lax.rem(self.mate - 2 * k + 2 * self.n, self.n)
-
-    def push_copy(self, k):
-        return self.copy(self.me, lax.rem(self.me + 2 * k, self.n), self.push_sem.at[k])
-
-    def mate_copy(self):
-        return self.copy(self.me, self.mate, self.push_sem.at[0])
-
-    def fwd_copy(self, k):
-        return self.copy(self.row(k), self.mate, self.fwd_sem.at[k])
-
-    def push(self):
-        self.mate_copy().start()
-
-        @pl.loop(1, self.half)
-        def _(k):
-            self.push_copy(k).start()
+    def row(self, i):
+        return 2 * i + self.side
+
+    def other(self, i):
+        return 2 * i + 1 - self.side
+
+    def right(self, i):
+        return self.copy(self.row(i), self.me + 2, self.right_sem.at[i])
+
+    def left(self, i):
+        return self.copy(self.row(i), self.me - 2, self.left_sem.at[i])
+
+    def to_mate(self, i):
+        return self.copy(self.row(i), self.mate, self.mate_sem.at[i])
+
+    def go_right(self, i):
+        @pl.when(self.at < self.last)
+        def _():
+            self.right(i).start()
+
+    def go_left(self, i):
+        @pl.when(self.at > 0)
+        def _():
+            self.left(i).start()
+
+    def begin(self):
+        self.go_right(self.at)
+        self.go_left(self.at)
+        self.to_mate(self.at).start()
 
     def wait_block(self, block):
-        self.copy(block, self.mate, self.fwd_sem.at[0]).wait_recv()
-
-    def forward(self):
-        @pl.loop(1, self.half)
-        def _(k):
-            self.wait_block(self.row(k))
-            self.fwd_copy(k).start()
+        self.copy(block, self.mate, self.mate_sem.at[0]).wait_recv()
+
+    def walk(self, visit_low, visit_high):
+        @pl.loop(1, self.last + 1)
+        def _(j):
+            @pl.when(self.at - j >= 0)
+            def _():
+                visit_low(self.at - j)
+
+            @pl.when(self.at + j <= self.last)
+            def _():
+                visit_high(self.at + j)
+
+    def relay(self, use=lambda block: None):
+        def low(i):
+            self.wait_block(self.row(i))
+            self.go_right(i)
+            self.to_mate(i).start()
+            use(self.row(i))
+
+        def high(i):
+            self.wait_block(self.row(i))
+            self.go_left(i)
+            self.to_mate(i).start()
+            use(self.row(i))
+
+        self.walk(low, high)
+
+    def each_row(self, use):
+        self.walk(lambda i: use(self.row(i)), lambda i: use(self.row(i)))
+
+    def each_other(self, use):
+        def visit(i):
+            self.wait_block(self.other(i))
+            use(self.other(i))
+
+        visit(self.at)
+        self.walk(visit, visit)
 
     def drain(self):
-        self.mate_copy().wait_send()
-
-        @pl.loop(1, self.half)
-        def _(k):
-            self.push_copy(k).wait_send()
-            self.fwd_copy(k).wait_send()
+        @pl.loop(0, self.last + 1)
+        def _(i):
+            self.to_mate(i).wait_send()
+
+            @pl.when(jnp.logical_and(self.at < self.last, i <= self.at))
+            def _():
+                self.right(i).wait_send()
+
+            @pl.when(jnp.logical_and(self.at > 0, i >= self.at))
+            def _():
+                self.left(i).wait_send()
 
 
 def kernel(
     n, layers, slot_row, slot_col, gate_col, x_ref, pre_ref, top_ref, up_ref, down_ref,
     gin_ref, gup_ref, gdown_ref,
     sg_all, up_all, xs_all, pre_all, slope_all, hid_all, part_mine, part_other, pg_all, pg_own, acc, inc,
-    sg_push, sg_fwd, sg_recv, up_push, up_fwd, up_recv, xs_push, xs_fwd, xs_recv,
+    sg_right, sg_left, sg_mate, sg_recv, up_right, up_left, up_mate, up_recv, xs_right, xs_left, xs_mate, xs_recv,
     pre_send, pre_recv, pre_mate_send, pre_mate_recv, part_send, part_recv, pg_send, pg_recv,
     down_send, down_recv,
 ):
@@ -87,9 +132,9 @@
     slots, half = x_ref.shape
     is_first = pair == layers - 1
 
-    sg = Gather(sg_all, sg_push, sg_fwd, sg_recv, me, n)
-    up = Gather(up_all, up_push, up_fwd, up_recv, me, n)
-    xs = Gather(xs_all, xs_push, xs_fwd, xs_recv, me, n)
+    sg = Gather(sg_all, sg_right, sg_left, sg_mate, sg_recv, me, n)
+    up = Gather(up_all, up_right, up_left, up_mate, up_recv, me, n)
+    xs = Gather(xs_all, xs_right, xs_left, xs_mate, xs_recv, me, n)
 
     barrier = pltpu.get_barrier_semaphore()
 
@@ -119,14 +164,17 @@
         make_slot_grad()
 
     up_all[me] = up_ref[...]
-    xs_all[me] = jnp.dot(onehot, x_ref[...], preferred_element_type=F32).astype(BF16)
 
     near_pairs = (pair > 0).astype(jnp.int32) + (pair < layers - 1).astype(jnp.int32)
     pl.semaphore_wait(barrier, n + near_pairs)
 
     @pl.when(is_first)
     def _():
-        sg.push()
+        sg.begin()
+
+    @pl.when(jnp.logical_not(is_first))
+    def _():
+        up.begin()
 
     owner_core = me // half_n
 
@@ -153,7 +201,9 @@
         def _():
             pre_copy(j).start()
 
-    up.push()
+    xs_all[me] = jnp.dot(onehot, x_ref[...], preferred_element_type=F32).astype(BF16)
+    gup_ref[...] = jnp.zeros_like(gup_ref)
+    gdown_ref[...] = jnp.zeros_like(gdown_ref)
 
     def take_pre():
         @pl.when(owner_core == core)
@@ -186,16 +236,16 @@
 
     @pl.when(jnp.logical_not(is_first))
     def _():
-        xs.push()
         take_pre()
-        up.forward()
-        xs.forward()
+        up.relay()
+        xs.begin()
+        xs.relay()
         pltpu.make_async_remote_copy(
             src_ref=gin_ref, dst_ref=inc, send_sem=down_send.at[0],
             recv_sem=down_recv.at[0], device_id={"section": sec + 2}, device_id_type=MESH,
         ).wait_recv()
         make_slot_grad()
-        sg.push()
+        sg.begin()
 
     def part_copy(b):
         return pltpu.make_async_remote_copy(
@@ -225,32 +275,46 @@
         def _():
             pg_copy(b).start()
 
+    def add_down(b):
+        gdown_ref[...] += lax.dot_general(hid_all[b], sg_all[b], TN, preferred_element_type=F32)
+
+    def add_up(b):
+        gup_ref[...] += lax.dot_general(pg_all[b], xs_all[b], TN, preferred_element_type=F32)
+
+    def finish_row(b):
+        finish_of(b)
+        add_down(b)
+
+        @pl.when(jnp.logical_not(is_first))
+        def _():
+            add_up(b)
+
+    def finish_other(b):
+        part_of(b)
+        add_down(b)
+        finish_of(b)
+
+        @pl.when(jnp.logical_not(is_first))
+        def _():
+            xs.wait_block(b)
+            add_up(b)
+
     part_of(me)
-
-    @pl.loop(1, half_n)
-    def _(k):
-        sg.wait_block(sg.row(k))
-        sg.fwd_copy(k).start()
-        part_of(sg.row(k))
+    sg.relay(part_of)
 
     @pl.when(is_first)
     def _():
+        up.begin()
         take_pre()
 
-    @pl.loop(0, half_n)
-    def _(k):
-        finish_of(sg.row(k))
-
-    @pl.loop(0, half_n)
-    def _(k):
-        sg.wait_block(sg.other(k))
-        part_of(sg.other(k))
-        finish_of(sg.other(k))
+    finish_row(me)
+    sg.each_row(finish_row)
+    sg.each_other(finish_other)
 
     @pl.when(is_first)
     def _():
-        up.forward()
-        xs.push()
+        up.relay()
+        xs.begin()
 
     def wait_pg(b):
         pltpu.make_async_remote_copy(
@@ -260,18 +324,12 @@
 
     acc[...] = jnp.dot(pg_own[me], up_all[me], preferred_element_type=F32)
 
-    @pl.loop(1, half_n)
-    def _(k):
-        b = up.row(k)
+    def add_acc(b):
         wait_pg(b)
         acc[...] += jnp.dot(pg_own[b], up_all[b], preferred_element_type=F32)
 
-    @pl.loop(0, half_n)
-    def _(k):
-        b = up.other(k)
-        up.wait_block(b)
-        wait_pg(b)
-        acc[...] += jnp.dot(pg_own[b], up_all[b], preferred_element_type=F32)
+    up.each_row(add_acc)
+    up.each_other(add_acc)
 
     onehot_t = (slot_col[...] == lax.broadcasted_iota(jnp.int32, (slots, slots), 1)).astype(BF16)
     delta = jnp.dot(onehot_t, acc[...].astype(BF16), preferred_element_type=F32)
@@ -283,22 +341,10 @@
 
     @pl.when(is_first)
     def _():
-        xs.forward()
-
-    def weight_grad(out_ref, left, right):
-        out_ref[...] = lax.dot_general(left[0], right[0], TN, preferred_element_type=F32)
-
-        @pl.loop(1, n)
-        def _(b):
-            out_ref[...] += lax.dot_general(left[b], right[b], TN, preferred_element_type=F32)
-
-    weight_grad(gdown_ref, hid_all, sg_all)
-
-    @pl.loop(0, half_n)
-    def _(k):
-        xs.wait_block(xs.other(k))
-
-    weight_grad(gup_ref, pg_all, xs_all)
+        xs.relay()
+        add_up(me)
+        xs.each_row(add_up)
+        xs.each_other(add_up)
 
     sg.drain()
     up.drain()
@@ -352,7 +398,7 @@
             thin(BF16), thin(F32), thin(BF16), thin(F32), thin(F32), thin(BF16), thin(BF16),
             pltpu.VMEM((slots, half), F32),
             pltpu.VMEM((slots, half), BF16),
-            dma(n // 2), dma(n // 2), dma(n), dma(n // 2), dma(n // 2), dma(n), dma(n // 2), dma(n // 2), dma(n),
+            *([dma(n // 2), dma(n // 2), dma(n // 2), dma(n)] * 3),
             dma(n // 2), dma(n), dma(1), dma(1), dma(n), dma(n), dma(n), dma(n),
             dma(1), dma(1),
         ],

time: 218 us -> 162 us (0.74)
  Pallas kernels: 209 us -> 152 us
    pallas_call x1, Pallas kernels: 209 us -> 152 us  [local(): pl.pallas_call(functools.partial(kernel, n, layers), out_shape=[jax.Shape...]
where the time goes in v2:
time: 162 us; the launch traced here: 161 us
  Pallas kernels  152 us (94%)
  local copies, waits for them, and re-layouts  8.6 us (5%)
    pallas_call x1, Pallas kernels, local(): pl.pallas_call(functools.partial(kernel, n, layers), out_shape=[jax.Shape...  152 us
    unnamed x12, local copies, waits for them, and re-layouts  5.1 us

profile of v2, /device:TPU:0, one launch (start us, length us, event | category | flops | bytes accessed | tf_op | source)
XLA Modules:
  0.0 161.5 jit_solution(831795185226458678)
XLA Ops:
  0.6 0.0 copy-start
  0.6 0.0 copy-start.3
  0.7 0.6 copy-done
  1.3 1.2 fusion
  2.6 0.7 copy.14.slot_col
  3.3 0.7 copy.15.gate_col
  4.0 0.0 copy-done.3
  4.0 0.1 copy.12
  4.2 0.8 copy.13
  4.9 152.2 %shard_map.94 = (bf16[128,1792]{1,0:T(8,128)(2,1)}, f32[128,1792]{1,0:T(8,128)}, f32[128,1792]{1,0:T(8,128)}) custom-call(s32[1,128]{1,0:T(1,128)} %get-tuple-element.10.slot_row, s32[128,1]{1,0:T(8,128)} %copy.14.slot_col, f32[128,1]{1,0:T(8,128)} %copy.15.gate_col, bf16[128,1792]{1,0:T(8,128)(2,1)} %bitcast.15, bf16[4,128,128]{2,1,0:T(8,128)(2,1)} %bitcast.12, ...), custom_call_target="tpu_custom_call" | custom-call | tf_op jit(solution)/shard_map/pallas_call | solution.py:387
  157.1 0.0 copy-start.2
  157.1 1.9 %copy.19 = bf16[1,128,1792]{2,1,0:T(8,128)(2,1)} copy(bf16[1,128,1792]{2,1,0:T(8,128)(2,1)} %bitcast.14) | data formatting | bytes 917504
  159.0 0.0 copy-done.2
  159.0 0.0 copy-start.1
  159.0 0.9 copy.20
  159.9 0.6 copy-done.1
  160.5 0.9 copy.21
  (1 shorter events, 0.0 us)
Async XLA Ops:
  0.6 0.7 copy-start
  0.6 3.4 %copy-start.3 = (bf16[1,128,512]{2,1,0:T(8,128)(2,1)S(1)}, bf16[1,128,512]{2,1,0:T(8,128)(2,1)}, u32[]{:S(2)}) copy-start(bf16[1,128,512]{2,1,0:T(8,128)(2,1)} %param.10) | copy-start | bytes 393220
  157.1 1.9 %copy-start.2 = (f32[128,1792]{1,0:T(8,128)S(1)}, f32[128,1792]{1,0:T(8,128)}, u32[]{:S(2)}) copy-start(f32[128,1792]{1,0:T(8,128)} %get-tuple-element.15) | copy-start | bytes 2752516
  159.0 1.5 copy-start.1

commit v3 on v2

--- a/solution.py
+++ b/solution.py
@@ -76,17 +76,19 @@
             def _():
                 visit_high(self.at + j)
 
-    def relay(self, use=lambda block: None):
+    def relay(self, use=lambda block: None, forward=True):
         def low(i):
             self.wait_block(self.row(i))
             self.go_right(i)
-            self.to_mate(i).start()
+            if forward:
+                self.to_mate(i).start()
             use(self.row(i))
 
         def high(i):
             self.wait_block(self.row(i))
             self.go_left(i)
-            self.to_mate(i).start()
+            if forward:
+                self.to_mate(i).start()
             use(self.row(i))
 
         self.walk(low, high)
@@ -120,9 +122,10 @@
     n, layers, slot_row, slot_col, gate_col, x_ref, pre_ref, top_ref, up_ref, down_ref,
     gin_ref, gup_ref, gdown_ref,
     sg_all, up_all, xs_all, pre_all, slope_all, hid_all, part_mine, part_other, pg_all, pg_own, acc, inc,
+    down_mate, pre_m, part2_mine, part2_other, pg_m,
     sg_right, sg_left, sg_mate, sg_recv, up_right, up_left, up_mate, up_recv, xs_right, xs_left, xs_mate, xs_recv,
     pre_send, pre_recv, pre_mate_send, pre_mate_recv, part_send, part_recv, pg_send, pg_recv,
-    down_send, down_recv,
+    down_send, down_recv, dm_send, dm_recv, pm_send, pm_recv, p2_send, p2_recv, pgx_send, pgx_recv, pg2_send,
 ):
     me = lax.axis_index("dp")
     sec = lax.axis_index("section")
@@ -168,8 +171,60 @@
     near_pairs = (pair > 0).astype(jnp.int32) + (pair < layers - 1).astype(jnp.int32)
     pl.semaphore_wait(barrier, n + near_pairs)
 
+    mate = sg.mate
+
+    def dm_copy():
+        return pltpu.make_async_remote_copy(
+            src_ref=down_ref, dst_ref=down_mate, send_sem=dm_send.at[0],
+            recv_sem=dm_recv.at[0], device_id={"dp": mate}, device_id_type=MESH,
+        )
+
+    def pm_copy(i):
+        return pltpu.make_async_remote_copy(
+            src_ref=pre_all.at[sg.other(i)], dst_ref=pre_m.at[i], send_sem=pm_send.at[i],
+            recv_sem=pm_recv.at[i], device_id={"dp": mate}, device_id_type=MESH,
+        )
+
+    def p2_copy(i):
+        return pltpu.make_async_remote_copy(
+            src_ref=part2_mine.at[i], dst_ref=part2_other.at[i], send_sem=p2_send.at[i],
+            recv_sem=p2_recv.at[i], device_id={"section": twin}, device_id_type=MESH,
+        )
+
+    def pgx_copy(i, block):
+        return pltpu.make_async_remote_copy(
+            src_ref=pg_m.at[i], dst_ref=pg_all.at[block], send_sem=pgx_send.at[i],
+            recv_sem=pgx_recv.at[i], device_id={"dp": mate}, device_id_type=MESH,
+        )
+
+    def pg2_copy(i):
+        return pltpu.make_async_remote_copy(
+            src_ref=pg_m.at[i], dst_ref=pg_own.at[mate], send_sem=pg2_send.at[i],
+            recv_sem=pg_recv.at[mate], device_id={"dp": sg.row(i)}, device_id_type=MESH,
+        )
+
+    def part2_of(i):
+        part2_mine[i] = lax.dot_general(sg_all[sg.row(i)], down_mate[...], NT, preferred_element_type=F32)
+        p2_copy(i).start()
+
+    def finish2(i):
+        p2_copy(i).wait_recv()
+        pm_copy(i).wait_recv()
+        slope = silu_slope(pre_m[i].astype(F32))
+        pg_m[i] = ((part2_mine[i] + part2_other[i]) * slope).astype(BF16)
+        pgx_copy(i, sg.row(i)).start()
+
+        @pl.when(i == sg.at)
+        def _():
+            pg_own[mate] = pg_m[i]
+
+        @pl.when(i != sg.at)
+        def _():
+            pg2_copy(i).start()
+
     @pl.when(is_first)
     def _():
+        dm_copy().start()
         sg.begin()
 
     @pl.when(jnp.logical_not(is_first))
@@ -293,28 +348,44 @@
         part_of(b)
         add_down(b)
         finish_of(b)
-
-        @pl.when(jnp.logical_not(is_first))
-        def _():
-            xs.wait_block(b)
-            add_up(b)
+        xs.wait_block(b)
+        add_up(b)
 
     part_of(me)
-    sg.relay(part_of)
+
+    @pl.when(jnp.logical_not(is_first))
+    def _():
+        sg.relay(part_of)
+
+    def both_parts(b):
+        part_of(b)
+        part2_of(b // 2)
 
     @pl.when(is_first)
     def _():
+        take_pre()
+
+        @pl.loop(0, half_n)
+        def _(i):
+            pm_copy(i).start()
+
+        dm_copy().wait_recv()
+        part2_of(sg.at)
+        sg.relay(both_parts, forward=False)
         up.begin()
-        take_pre()
+        finish2(sg.at)
+        sg.each_row(lambda b: finish2(b // 2))
 
     finish_row(me)
     sg.each_row(finish_row)
-    sg.each_other(finish_other)
+
+    @pl.when(jnp.logical_not(is_first))
+    def _():
+        sg.each_other(finish_other)
 
     @pl.when(is_first)
     def _():
         up.relay()
-        xs.begin()
 
     def wait_pg(b):
         pltpu.make_async_remote_copy(
@@ -325,7 +396,10 @@
     acc[...] = jnp.dot(pg_own[me], up_all[me], preferred_element_type=F32)
 
     def add_acc(b):
-        wait_pg(b)
+        @pl.when(jnp.logical_not(jnp.logical_and(is_first, b == mate)))
+        def _():
+            wait_pg(b)
+
         acc[...] += jnp.dot(pg_own[b], up_all[b], preferred_element_type=F32)
 
     up.each_row(add_acc)
@@ -341,10 +415,18 @@
 
     @pl.when(is_first)
     def _():
+        xs.begin()
+        sg.each_row(lambda b: sg.to_mate(b // 2).start())
         xs.relay()
         add_up(me)
         xs.each_row(add_up)
-        xs.each_other(add_up)
+        sg.each_other(add_down)
+
+        def add_up_other(b):
+            pgx_copy(b // 2, b).wait_recv()
+            add_up(b)
+
+        xs.each_other(add_up_other)
 
     sg.drain()
     up.drain()
@@ -360,13 +442,34 @@
     def _():
         pre_mate_copy().wait_send()
 
-    @pl.loop(0, n)
-    def _(b):
+    def drain_parts(b):
         part_copy(b).wait_send()
 
         @pl.when(b != me)
         def _():
             pg_copy(b).wait_send()
+
+    @pl.loop(0, half_n)
+    def _(i):
+        drain_parts(sg.row(i))
+
+        @pl.when(jnp.logical_not(is_first))
+        def _():
+            drain_parts(sg.other(i))
+
+        @pl.when(is_first)
+        def _():
+            pm_copy(i).wait_send()
+            p2_copy(i).wait_send()
+            pgx_copy(i, sg.row(i)).wait_send()
+
+            @pl.when(i != sg.at)
+            def _():
+                pg2_copy(i).wait_send()
+
+    @pl.when(is_first)
+    def _():
+        dm_copy().wait_send()
 
     @pl.when(pair > 0)
     def _():
@@ -384,6 +487,7 @@
     dma = lambda count: pltpu.SemaphoreType.DMA((count,))
     wide = pltpu.VMEM((n, slots, half), BF16)
     thin = lambda dtype: pltpu.VMEM((n, slots, units), dtype)
+    thin2 = lambda dtype: pltpu.VMEM((n // 2, slots, units), dtype)
     gin, gup, gdown = pl.pallas_call(
         functools.partial(kernel, n, layers),
         out_shape=[
@@ -398,9 +502,10 @@
             thin(BF16), thin(F32), thin(BF16), thin(F32), thin(F32), thin(BF16), thin(BF16),
             pltpu.VMEM((slots, half), F32),
             pltpu.VMEM((slots, half), BF16),
+            pltpu.VMEM((units, half), BF16), thin2(BF16), thin2(F32), thin2(F32), thin2(BF16),
             *([dma(n // 2), dma(n // 2), dma(n // 2), dma(n)] * 3),
             dma(n // 2), dma(n), dma(1), dma(1), dma(n), dma(n), dma(n), dma(n),
-            dma(1), dma(1),
+            dma(1), dma(1), dma(1), dma(1), *([dma(n // 2)] * 7),
         ],
         compiler_params=pltpu.CompilerParams(
             collective_id=0, has_side_effects=True, vmem_limit_bytes=62 * 1024 * 1024

time: 162 us -> 184 us (1.14)
  the two profiles are of different devices: /device:TPU:0 before, /device:TPU:2 now
where the time goes in v3:
time: 184 us; the launch traced here: 183 us
  Pallas kernels  174 us (95%)
  local copies, waits for them, and re-layouts  8.6 us (5%)
    pallas_call x1, Pallas kernels, local(): pl.pallas_call(functools.partial(kernel, n, layers), out_shape=[jax.Shape...  174 us
    unnamed x12, local copies, waits for them, and re-layouts  5.1 us

profile of v3, /device:TPU:2, one launch (start us, length us, event | category | flops | bytes accessed | tf_op | source)
XLA Modules:
  0.0 183.5 jit_solution(10538455325891349362)
XLA Ops:
  0.6 0.0 copy-start
  0.6 0.0 copy-start.3
  0.7 0.6 copy-done
  1.3 1.2 fusion
  2.6 0.7 copy.14.slot_col
  3.3 0.7 copy.15.gate_col
  4.0 0.0 copy-done.3
  4.0 0.1 copy.12
  4.2 0.8 copy.13
  4.9 174.2 %shard_map.94 = (bf16[128,1792]{1,0:T(8,128)(2,1)}, f32[128,1792]{1,0:T(8,128)}, f32[128,1792]{1,0:T(8,128)}) custom-call(s32[1,128]{1,0:T(1,128)} %get-tuple-element.10.slot_row, s32[128,1]{1,0:T(8,128)} %copy.14.slot_col, f32[128,1]{1,0:T(8,128)} %copy.15.gate_col, bf16[128,1792]{1,0:T(8,128)(2,1)} %bitcast.15, bf16[4,128,128]{2,1,0:T(8,128)(2,1)} %bitcast.12, ...), custom_call_target="tpu_custom_call" | custom-call | tf_op jit(solution)/shard_map/pallas_call | solution.py:491
  179.1 0.0 copy-start.2
  179.2 1.9 %copy.19 = bf16[1,128,1792]{2,1,0:T(8,128)(2,1)} copy(bf16[1,128,1792]{2,1,0:T(8,128)(2,1)} %bitcast.14) | data formatting | bytes 917504
  181.1 0.0 copy-done.2
  181.1 0.0 copy-start.1
  181.1 0.9 copy.20
  182.0 0.6 copy-done.1
  182.6 0.9 copy.21
  (1 shorter events, 0.0 us)
Async XLA Ops:
  0.6 0.7 copy-start
  0.6 3.4 %copy-start.3 = (bf16[1,128,512]{2,1,0:T(8,128)(2,1)S(1)}, bf16[1,128,512]{2,1,0:T(8,128)(2,1)}, u32[]{:S(2)}) copy-start(bf16[1,128,512]{2,1,0:T(8,128)(2,1)} %param.10) | copy-start | bytes 393220
  179.1 1.9 %copy-start.2 = (f32[128,1792]{1,0:T(8,128)S(1)}, f32[128,1792]{1,0:T(8,128)}, u32[]{:S(2)}) copy-start(f32[128,1792]{1,0:T(8,128)} %get-tuple-element.15) | copy-start | bytes 2752516
  181.1 1.5 copy-start.1

commit v4 on v3

--- a/solution.py
+++ b/solution.py
@@ -222,15 +222,6 @@
         def _():
             pg2_copy(i).start()
 
-    @pl.when(is_first)
-    def _():
-        dm_copy().start()
-        sg.begin()
-
-    @pl.when(jnp.logical_not(is_first))
-    def _():
-        up.begin()
-
     owner_core = me // half_n
 
     def pre_copy(j):
@@ -255,6 +246,15 @@
         @pl.when(core * half_n + j != me)
         def _():
             pre_copy(j).start()
+
+    @pl.when(is_first)
+    def _():
+        dm_copy().start()
+        sg.begin()
+
+    @pl.when(jnp.logical_not(is_first))
+    def _():
+        up.begin()
 
     xs_all[me] = jnp.dot(onehot, x_ref[...], preferred_element_type=F32).astype(BF16)
     gup_ref[...] = jnp.zeros_like(gup_ref)
@@ -357,24 +357,25 @@
     def _():
         sg.relay(part_of)
 
-    def both_parts(b):
-        part_of(b)
-        part2_of(b // 2)
-
     @pl.when(is_first)
     def _():
+        sg.relay(part_of, forward=False)
         take_pre()
 
         @pl.loop(0, half_n)
         def _(i):
             pm_copy(i).start()
 
+        up.begin()
         dm_copy().wait_recv()
-        part2_of(sg.at)
-        sg.relay(both_parts, forward=False)
-        up.begin()
-        finish2(sg.at)
-        sg.each_row(lambda b: finish2(b // 2))
+
+        @pl.loop(0, half_n)
+        def _(i):
+            part2_of(i)
+
+        @pl.loop(0, half_n)
+        def _(i):
+            finish2(i)
 
     finish_row(me)
     sg.each_row(finish_row)

time: 184 us -> 177 us (0.962)
  Pallas kernels: 174 us -> 167 us
    pallas_call x1, Pallas kernels: 174 us -> 167 us  [local(): pl.pallas_call(functools.partial(kernel, n, layers), out_shape=[jax.Shape...]
where the time goes in v4:
time: 177 us
  Pallas kernels  167 us (94%)
  local copies, waits for them, and re-layouts  8.6 us (5%)
    pallas_call x1, Pallas kernels, local(): pl.pallas_call(functools.partial(kernel, n, layers), out_shape=[jax.Shape...  167 us
    unnamed x12, local copies, waits for them, and re-layouts  5.1 us

profile of v4, /device:TPU:2, one launch (start us, length us, event | category | flops | bytes accessed | tf_op | source)
XLA Modules:
  0.0 176.8 jit_solution(10072813302329004424)
XLA Ops:
  0.6 0.0 copy-start
  0.6 0.0 copy-start.3
  0.7 0.6 copy-done
  1.3 1.2 fusion
  2.6 0.7 copy.14.slot_col
  3.3 0.7 copy.15.gate_col
  4.0 0.0 copy-done.3
  4.0 0.1 copy.12
  4.2 0.8 copy.13
  4.9 167.5 %shard_map.94 = (bf16[128,1792]{1,0:T(8,128)(2,1)}, f32[128,1792]{1,0:T(8,128)}, f32[128,1792]{1,0:T(8,128)}) custom-call(s32[1,128]{1,0:T(1,128)} %get-tuple-element.10.slot_row, s32[128,1]{1,0:T(8,128)} %copy.14.slot_col, f32[128,1]{1,0:T(8,128)} %copy.15.gate_col, bf16[128,1792]{1,0:T(8,128)(2,1)} %bitcast.15, bf16[4,128,128]{2,1,0:T(8,128)(2,1)} %bitcast.12, ...), custom_call_target="tpu_custom_call" | custom-call | tf_op jit(solution)/shard_map/pallas_call | solution.py:492
  172.4 0.0 copy-start.2
  172.4 1.9 %copy.19 = bf16[1,128,1792]{2,1,0:T(8,128)(2,1)} copy(bf16[1,128,1792]{2,1,0:T(8,128)(2,1)} %bitcast.14) | data formatting | bytes 917504
  174.3 0.0 copy-done.2
  174.3 0.0 copy-start.1
  174.3 0.9 copy.20
  175.2 0.6 copy-done.1
  175.8 0.9 copy.21
  (1 shorter events, 0.0 us)
Async XLA Ops:
  0.6 0.7 copy-start
  0.6 3.4 %copy-start.3 = (bf16[1,128,512]{2,1,0:T(8,128)(2,1)S(1)}, bf16[1,128,512]{2,1,0:T(8,128)(2,1)}, u32[]{:S(2)}) copy-start(bf16[1,128,512]{2,1,0:T(8,128)(2,1)} %param.10) | copy-start | bytes 393220
  172.4 1.9 %copy-start.2 = (f32[128,1792]{1,0:T(8,128)S(1)}, f32[128,1792]{1,0:T(8,128)}, u32[]{:S(2)}) copy-start(f32[128,1792]{1,0:T(8,128)} %get-tuple-element.15) | copy-start | bytes 2752516
  174.3 1.5 copy-start.1

commit v5 on v4

--- a/solution.py
+++ b/solution.py
@@ -367,6 +367,7 @@
             pm_copy(i).start()
 
         up.begin()
+        up.relay()
         dm_copy().wait_recv()
 
         @pl.loop(0, half_n)
@@ -384,9 +385,6 @@
     def _():
         sg.each_other(finish_other)
 
-    @pl.when(is_first)
-    def _():
-        up.relay()
 
     def wait_pg(b):
         pltpu.make_async_remote_copy(

time: 177 us -> 176 us (level)
  no operation moved by 1% of the time
where the time goes in v5:
time: 176 us
  Pallas kernels  167 us (95%)
  local copies, waits for them, and re-layouts  8.6 us (5%)
    pallas_call x1, Pallas kernels, local(): pl.pallas_call(functools.partial(kernel, n, layers), out_shape=[jax.Shape...  167 us
    unnamed x12, local copies, waits for them, and re-layouts  5.1 us

profile of v5, /device:TPU:2, one launch (start us, length us, event | category | flops | bytes accessed | tf_op | source)
XLA Modules:
  0.0 176.0 jit_solution(6359560140230557094)
XLA Ops:
  0.6 0.0 copy-start
  0.6 0.0 copy-start.3
  0.7 0.6 copy-done
  1.3 1.2 fusion
  2.6 0.7 copy.14.slot_col
  3.3 0.7 copy.15.gate_col
  4.0 0.0 copy-done.3
  4.0 0.1 copy.12
  4.2 0.8 copy.13
  4.9 166.7 %shard_map.94 = (bf16[128,1792]{1,0:T(8,128)(2,1)}, f32[128,1792]{1,0:T(8,128)}, f32[128,1792]{1,0:T(8,128)}) custom-call(s32[1,128]{1,0:T(1,128)} %get-tuple-element.10.slot_row, s32[128,1]{1,0:T(8,128)} %copy.14.slot_col, f32[128,1]{1,0:T(8,128)} %copy.15.gate_col, bf16[128,1792]{1,0:T(8,128)(2,1)} %bitcast.15, bf16[4,128,128]{2,1,0:T(8,128)(2,1)} %bitcast.12, ...), custom_call_target="tpu_custom_call" | custom-call | tf_op jit(solution)/shard_map/pallas_call | solution.py:490
  171.7 0.0 copy-start.2
  171.7 1.9 %copy.19 = bf16[1,128,1792]{2,1,0:T(8,128)(2,1)} copy(bf16[1,128,1792]{2,1,0:T(8,128)(2,1)} %bitcast.14) | data formatting | bytes 917504
  173.6 0.0 copy-done.2
  173.6 0.0 copy-start.1
  173.6 0.9 copy.20
  174.5 0.6 copy-done.1
  175.1 0.9 copy.21
  (1 shorter events, 0.0 us)
Async XLA Ops:
  0.6 0.7 copy-start
  0.6 3.4 %copy-start.3 = (bf16[1,128,512]{2,1,0:T(8,128)(2,1)S(1)}, bf16[1,128,512]{2,1,0:T(8,128)(2,1)}, u32[]{:S(2)}) copy-start(bf16[1,128,512]{2,1,0:T(8,128)(2,1)} %param.10) | copy-start | bytes 393220
  171.7 1.9 %copy-start.2 = (f32[128,1792]{1,0:T(8,128)S(1)}, f32[128,1792]{1,0:T(8,128)}, u32[]{:S(2)}) copy-start(f32[128,1792]{1,0:T(8,128)} %get-tuple-element.15) | copy-start | bytes 2752516
  173.6 1.5 copy-start.1
